TPU v7x, 32 devices: a whole 2x2x4 slice. The times are simulated.
32 devices in a mesh: groups: 2 (over y), ctx: 4 (over z), ep: 2 (over x), tp: 2 (over core).
Axes of the slice: x: 2, y: 2, z: 4, core: 2. Of those that a mesh axis runs over, the one named last changes fastest.
Arguments:
- queries: bfloat16 [4, 512, 5120], P(('groups', 'ep'), 'ctx', 'tp'), parts along dimension 0, may hold values from -128 to 128
- keys: bfloat16 [4, 512, 1024], P(('groups', 'ep'), 'ctx', 'tp'), parts along dimension 0, may hold values from -6 to 6
- values: bfloat16 [4, 512, 1024], P(('groups', 'ep'), 'ctx', 'tp'), parts along dimension 0, may hold values from -6 to 6
- expert_ids: int32 [4, 512, 1], P(('groups', 'ep'), 'ctx'), parts along dimension 0, may hold values from 0 to 127, as said below
- router: bfloat16 [5120, 2], P('tp', 'ep'), may hold values from -0.3125 to 0.3125
- w_gate: bfloat16 [2, 5120, 4096], P('ep', 'tp', 'ctx'), may hold values from -0.3125 to 0.3125
- w_up: bfloat16 [2, 5120, 4096], P('ep', 'tp', 'ctx'), may hold values from -0.3125 to 0.3125
- w_down: bfloat16 [2, 4096, 5120], P('ep', 'ctx', 'tp'), may hold values from -0.09375 to 0.09375
Outputs:
- layer_out: bfloat16 [4, 512, 5120], P(('groups', 'ep'), 'ctx', 'tp'), parts along dimension 0
There are 2 independent parts, one for each index of `groups`. A program takes and returns all parts, laid end to end along the dimension named above; an argument that names none is the same for every part. Nothing has to cross between parts.
Inputs may be any that keep to these rules, and one draw needn't show every extreme that they name: `expert_ids`: among the positions of one device, each expert below 2 is named at most 2 times; in every draw one of them is named exactly 2 times on every device.
All inputs are finite; a program needn't handle non-finite values.
Results may differ from a plain program's by a relative error of at most 0.023.
Values may be sent and summed in bfloat16 or wider, within the bound.
A program may use at most 64 MiB of HBM per device.

v0:
```python
import jax
import jax.numpy as jnp
from jax import lax
from jax.sharding import PartitionSpec as P

HEAD_WIDTH = 128
CAP = 2


def block_width(key_count):
    for candidate in (512, 256, 128):
        return candidate
    return key_count


def fresh_state(query_rows, kv_heads, group_width):
    return (
        jnp.full((kv_heads, group_width, query_rows), -1e30, jnp.float32),
        jnp.zeros((kv_heads, group_width, query_rows), jnp.float32),
        jnp.zeros((query_rows, kv_heads, group_width, HEAD_WIDTH), jnp.float32),
    )


def absorb_block(status, query_half, query_pos, key_block, value_block, key_pos):
    old_max, totals, weighted = status
    scores = jnp.einsum(
        "rgqd,kgd->gqrk", query_half, key_block, preferred_element_type=jnp.float32
    ) * HEAD_WIDTH ** (-0.5)
    visible = query_pos[:, None] >= key_pos[None, :]
    scores = jnp.where(visible, scores, -1e30)
    running_max = jnp.maximum(old_max, jnp.max(scores, axis=3))
    factor = jnp.exp(old_max - running_max)
    weights = jnp.where(visible, jnp.exp(scores - running_max[..., None]), 0.0)
    totals = totals * factor + jnp.sum(weights, axis=3)
    update = jnp.einsum(
        "gqrk,kgd->rgqd",
        weights.astype(jnp.bfloat16),
        value_block,
        preferred_element_type=jnp.float32,
    )
    weighted = weighted * jnp.transpose(factor, (2, 0, 1))[..., None] + update
    return (running_max, totals, weighted)


def finish(status, row_count):
    old_max, totals, weighted = status
    normed = weighted / jnp.transpose(totals, (2, 0, 1))[..., None]
    return normed.astype(jnp.bfloat16).reshape(row_count, -1)


def shards(queries, keys, values, expert_ids, router, w_gate, w_up, w_down):
    row_count = queries.shape[1]
    half_rows = row_count // 2
    feature_width = queries.shape[2]
    kv_heads = keys.shape[2] // HEAD_WIDTH
    group_width = feature_width // HEAD_WIDTH // kv_heads
    ep_count = lax.axis_size("ep")
    ctx_place = lax.axis_index("ctx")
    local_queries = queries[0].reshape(row_count, kv_heads, group_width, HEAD_WIDTH)
    lead_half = local_queries[:half_rows]
    tail_half = local_queries[half_rows:]
    lead_pos = ctx_place * row_count + jnp.arange(half_rows, dtype=jnp.int32)
    tail_pos = ctx_place * row_count + half_rows + jnp.arange(half_rows, dtype=jnp.int32)
    initial = (
        fresh_state(half_rows, kv_heads, group_width),
        fresh_state(half_rows, kv_heads, group_width),
    )
    key_piece = lax.all_gather(keys, "ctx", axis=1, tiled=True)[0]
    key_count = key_piece.shape[0]
    key_block_rows = block_width(key_count)
    block_count = key_count // key_block_rows
    key_blocks = key_piece.reshape(block_count, key_block_rows, kv_heads, HEAD_WIDTH)
    value_blocks = lax.all_gather(values, "ctx", axis=1, tiled=True)[0].reshape(
        block_count, key_block_rows, kv_heads, HEAD_WIDTH
    )
    offsets = jnp.arange(block_count, dtype=jnp.int32) * key_block_rows

    def one_block(status, inputs):
        key_block, value_block, block_begin = inputs
        key_pos = block_begin + jnp.arange(key_block_rows, dtype=jnp.int32)
        lead_state = lax.cond(
            block_begin <= lead_pos[-1],
            lambda kept_state: absorb_block(
                kept_state, lead_half, lead_pos, key_block, value_block, key_pos
            ),
            lambda kept_state: kept_state,
            status[0],
        )
        tail_state = lax.cond(
            block_begin <= tail_pos[-1],
            lambda kept_state: absorb_block(
                kept_state, tail_half, tail_pos, key_block, value_block, key_pos
            ),
            lambda kept_state: kept_state,
            status[1],
        )
        return ((lead_state, tail_state), None)

    result, _ = lax.scan(one_block, initial, (key_blocks, value_blocks, offsets))
    lead_status, tail_status = result
    lead_out = finish(lead_status, half_rows)
    tail_out = finish(tail_status, half_rows)
    attended = jnp.concatenate([lead_out, tail_out], axis=0)
    chosen = expert_ids[0, :, 0]
    choose = (chosen[:, None] == jnp.arange(ep_count, dtype=jnp.int32)[None, :]).astype(jnp.int32)
    earlier = jnp.cumsum(choose, axis=0) - choose
    slot_index = jnp.sum(earlier * choose, axis=1)
    target = chosen * CAP + slot_index
    spread = (target[None, :] == jnp.arange(ep_count * CAP, dtype=jnp.int32)[:, None]).astype(
        jnp.bfloat16
    )
    outgoing = jnp.dot(spread, attended, preferred_element_type=jnp.float32).astype(jnp.bfloat16)
    arrived = lax.all_to_all(
        outgoing.reshape(ep_count, CAP, feature_width),
        "ep",
        split_axis=0,
        concat_axis=0,
        tiled=True,
    )
    gathered = lax.all_gather(arrived[None], "ctx", axis=0, tiled=True)
    members = gathered.reshape(-1, feature_width)
    gate_w = w_gate[0]
    up_w = w_up[0]
    down_w = w_down[0]
    gate_part = jnp.dot(members, gate_w, preferred_element_type=jnp.float32)
    up_part = jnp.dot(members, up_w, preferred_element_type=jnp.float32)
    score_part = jnp.dot(members, router, preferred_element_type=jnp.float32)
    gate_sum, up_sum, router_score = (
        lax.psum(gate_part.astype(jnp.bfloat16), "tp").astype(jnp.float32),
        lax.psum(up_part.astype(jnp.bfloat16), "tp").astype(jnp.float32),
        lax.psum(score_part.astype(jnp.bfloat16), "tp").astype(jnp.float32),
    )
    weight = jax.nn.sigmoid(router_score)
    hidden = (jax.nn.silu(weight * gate_sum) * (weight * up_sum)).astype(jnp.bfloat16)
    expert_rows = lax.psum_scatter(
        jnp.dot(hidden, down_w, preferred_element_type=jnp.float32).astype(jnp.bfloat16),
        "ctx",
        scatter_dimension=0,
        tiled=True,
    )
    returned = lax.all_to_all(
        expert_rows.reshape(ep_count, CAP, feature_width),
        "ep",
        split_axis=0,
        concat_axis=0,
        tiled=True,
    )
    returned = returned.reshape(ep_count * CAP, feature_width)
    routed = lax.dot_general(
        spread, returned, (((0,), (0,)), ((), ())), preferred_element_type=jnp.float32
    )
    layer_out = (attended.astype(jnp.float32) + routed).astype(jnp.bfloat16)
    return layer_out[None]


def solution(mesh):
    placed = (
        P(("groups", "ep"), "ctx", "tp"),
        P(("groups", "ep"), "ctx", "tp"),
        P(("groups", "ep"), "ctx", "tp"),
        P(("groups", "ep"), "ctx", None),
        P("tp", "ep"),
        P("ep", "tp", "ctx"),
        P("ep", "tp", "ctx"),
        P("ep", "ctx", "tp"),
    )
    return jax.shard_map(
        shards,
        mesh=mesh,
        in_specs=placed,
        out_specs=P(("groups", "ep"), "ctx", "tp"),
        check_vma=False,
    )
```

profile of v0, /device:TPU:0, one launch (start us, length us, event | category | flops | bytes accessed | tf_op | source)
XLA Modules:
  0.0 157.5 jit_solution(6667889364840034550)
XLA Ops:
  6.5 1.0 copy.23
  7.6 16.7 %all_gather.9 = bf16[1,512,512]{1,2,0:T(8,128)(2,1)S(1)} all-gather(bf16[1,128,512]{1,2,0:T(8,128)(2,1)S(1)} %copy.23), channel_id=1, replica_groups=mesh['groups'=2,'ctx'=4,'ep'=2,'tp'=2] {'ctx'}, dimensions={1}, use_global_device_ids=true | all-gather | bytes 655360 | tf_op jit(solution)/shard_map/all_gather | solution.py:68
  24.3 1.0 copy.24
  25.3 14.6 %all_gather.10 = bf16[1,512,512]{1,2,0:T(8,128)(2,1)S(1)} all-gather(bf16[1,128,512]{1,2,0:T(8,128)(2,1)S(1)} %copy.24), channel_id=1, replica_groups=mesh['groups'=2,'ctx'=4,'ep'=2,'tp'=2] {'ctx'}, dimensions={1}, use_global_device_ids=true | all-gather | bytes 655360 | tf_op jit(solution)/shard_map/all_gather | solution.py:73
  39.9 0.6 slice.23
  41.1 0.1 broadcast.44
  41.2 0.6 broadcast.43
  41.8 4.8 %conditional.3 = (f32[4,5,64]{2,1,0:T(8,128)S(1)}, f32[64,4,5,128]{3,0,2,1:T(8,128)S(1)}) conditional(s32[]{:T(128)} %bitcast.14, (f32[4,5,64]{2,1,0:T(8,128)}, f32[64,4,5,128]{3,0,2,1:T(8,128)S(1)}) %tuple.31, (s32[64]{0:T(128)S(1)}, s32[512]{0:T(512)S(1)}, bf16[1,128,2560]{2,1,0:T(8,128)(2,1)}, bf16[512,4,128]{0,2,1:T(8,128)(2,1)S(1)}, ...), branch_computations={%region_4.5_spmd, %region_5.0_spmd} | conditional | flops 344428288 | bytes 12067088 | solution.py:89
  41.8 0.1 broadcast_compare_fusion.1
  41.9 1.0 slice.18
  42.9 0.4 slice.19
  43.3 0.7 fusion.20
  44.0 0.9 fusion.22
  44.9 0.7 multiply_add_fusion.1
  45.6 1.1 fusion.29
  46.7 0.2 divide_convert_fusion
  46.9 0.2 copy.30
  47.2 0.4 reshape.57
  47.6 0.6 slice.22
  48.8 5.9 %conditional.2 = ((f32[4,5,64]{2,1,0:T(8,128)}, f32[64,4,5,128]{3,0,2,1:T(8,128)S(1)})) conditional(s32[]{:T(128)} %bitcast.10, (f32[4,5,64]{2,1,0:T(8,128)}, f32[64,4,5,128]{3,0,2,1:T(8,128)S(1)}) %tuple.31, (s32[64]{0:T(128)S(1)}, s32[512]{0:T(512)S(1)}, bf16[1,128,2560]{2,1,0:T(8,128)(2,1)S(1)}, bf16[512,4,128]{0,2,1:T(8,128)(2,1)S(1)}, ...), branch_computations={%region_0.1_spmd, %region_1.4_spmd} | conditional | flops 344428288 | bytes 12239212 | solution.py:81
  48.8 0.7 broadcast_compare_fusion
  49.6 0.4 slice.17
  50.0 1.4 fusion
  51.4 0.9 fusion.2
  52.3 1.3 multiply_add_fusion
  53.6 1.1 fusion.9
  54.7 1.0 divide_convert_fusion.1
  55.7 0.2 copy.27
  55.9 0.4 reshape.56
  56.4 0.1 fusion.59
  56.4 0.2 reduce_window_sum.11
  56.6 0.2 select_reduce_fusion
  56.8 0.2 convolution_convert_fusion
  57.1 6.4 %all_to_all.10 = bf16[2,2,2560]{2,1,0:T(2,128)(2,1)S(1)} all-to-all(bf16[2,2,2560]{2,1,0:T(2,128)(2,1)S(1)} %reshape.58), channel_id=1, replica_groups=mesh['groups'=2,'ctx'=4,'ep'=2,'tp'=2] {'ep'}, dimensions={0} | all-to-all | bytes 40960 | tf_op jit(solution)/shard_map/all_to_all | solution.py:113
  63.5 13.2 %all-gather = bf16[8,2,2560]{2,1,0:T(2,128)(2,1)S(1)} all-gather(bf16[2,2,2560]{2,1,0:T(2,128)(2,1)S(1)} %all_to_all.10), channel_id=2, replica_groups=mesh['groups'=2,'ctx'=4,'ep'=2,'tp'=2] {'ctx'}, dimensions={0}, use_global_device_ids=true | all-gather | bytes 102400 | tf_op jit(solution)/shard_map/all_gather | solution.py:120
  76.7 3.9 %fusion.51 = bf16[16,1024]{1,0:T(8,128)(2,1)} fusion(bf16[16,2560]{1,0:T(8,128)(2,1)S(1)} %reshape.59, bf16[1,2560,1024]{2,1,0:T(8,128)(2,1)} %param.17), kind=kOutput, calls=%fused_computation.51 | convolution fusion | flops 83902464 | bytes 5357568 | tf_op jit(solution)/shard_map/dot_general | solution.py:125
  80.6 3.9 %fusion.54 = bf16[16,1024]{1,0:T(8,128)(2,1)} fusion(bf16[16,2560]{1,0:T(8,128)(2,1)S(1)} %reshape.59, bf16[1,2560,1024]{2,1,0:T(8,128)(2,1)} %param.18), kind=kOutput, calls=%fused_computation.52 | convolution fusion | flops 83902464 | bytes 5357568 | tf_op jit(solution)/shard_map/dot_general | solution.py:126
  84.6 0.6 fusion.58
  85.2 0.0 all-reduce.7.cloned.1.call-update
  85.2 0.0 all-reduce.5.cloned.1.call-start
  85.3 16.5 %all-reduce.7.cloned.1.call-done = (bf16[16,1024]{1,0:T(8,128)(2,1)}, bf16[16,1024]{1,0:T(8,128)(2,1)}, bf16[16,1]{0,1:T(2,128)(2,1)}) async-done(((bf16[16,1024]{1,0:T(8,128)(2,1)}, bf16[16,1024]{1,0:T(8,128)(2,1)}, bf16[16,1]{0,1:T(2,128)(2,1)}), (bf16[16,1024]{1,0:T(8,128)(2,1)}, bf16[16,1024]{1,0:T(8,128)(2,1)}, bf16[16,1]{0,1:T(2,128)(2,1)})) %all-reduce.7.cloned.1.call-update) | async-done | bytes 65584 | tf_op jit(solution)/shard_map/psum | solution.py:130
  101.8 0.7 divide_bitcast_fusion
  102.5 4.0 %fusion.48 = bf16[16,2560]{1,0:T(8,128)(2,1)} fusion(bf16[1,1024,2560]{2,1,0:T(8,128)(2,1)} %param.19, bf16[16,1024]{1,0:T(8,128)(2,1)} %get-tuple-element.178, bf16[16,1024]{1,0:T(8,128)(2,1)} %get-tuple-element.179, f32[16]{0:T(128)S(1)} %divide_bitcast_fusion), kind=kOutput, calls=%fused_computation.49 | convolution fusion | flops 84090880 | bytes 5390400 | tf_op jit(solution)/shard_map/dot_general | solution.py:136
  106.6 0.6 dynamic-slice
  107.7 34.5 %all-reduce.5.cloned.1.call-done = bf16[16,2560]{1,0:T(8,128)(2,1)} async-done(((bf16[16,2560]{1,0:T(8,128)(2,1)}), bf16[16,2560]{1,0:T(8,128)(2,1)}) %all-reduce.5.cloned.1.call-update) | async-done | bytes 81936
  142.2 0.8 constant_dynamic-slice_fusion
  143.0 6.4 %all_to_all.11 = bf16[2,2,2560]{2,1,0:T(2,128)(2,1)S(1)} all-to-all(bf16[2,2,2560]{2,1,0:T(2,128)(2,1)S(1)} %reshape.61), channel_id=1, replica_groups=mesh['groups'=2,'ctx'=4,'ep'=2,'tp'=2] {'ep'}, dimensions={0} | all-to-all | bytes 40960 | tf_op jit(solution)/shard_map/all_to_all | solution.py:141
  149.5 1.2 fusion.47
  (31 shorter events, 0.3 us)
Async XLA Ops:
  6.5 78.0 %copy-start = (bf16[2560,1]{0,1:T(2,128)(2,1)S(1)}, bf16[2560,1]{0,1:T(2,128)(2,1)}, u32[]{:S(2)}) copy-start(bf16[2560,1]{0,1:T(2,128)(2,1)} %param.16) | copy-start | bytes 15364
  6.5 95.3 %all-reduce.7.cloned.1.call-start = ((), (), s32[]{:S(2)}) async-start(), calls=%async_computation.3 | async-start | bytes 132096 | tf_op jit(solution)/shard_map/psum | solution.py:130
  46.7 2.1 %copy-start.1 = (bf16[1,128,2560]{2,1,0:T(8,128)(2,1)S(1)}, bf16[1,128,2560]{2,1,0:T(8,128)(2,1)}, u32[]{:S(2)}) copy-start(bf16[1,128,2560]{2,1,0:T(8,128)(2,1)} %param.12) | copy-start | bytes 1966084
  48.8 0.7 copy-start.2
  49.6 1.8 %copy-start.3 = (f32[4,5,64]{2,1,0:T(8,128)S(1)}, f32[4,5,64]{2,1,0:T(8,128)}, u32[]{:S(2)}) copy-start(f32[4,5,64]{2,1,0:T(8,128)} %copy-done.2) | copy-start | bytes 15364 | tf_op jit(solution)/shard_map/while/body/eval_jaxpr/cond
  49.6 1.9 %copy-start.4 = (pred[64,512]{1,0:T(8,128)(4,1)S(1)}, pred[64,512]{1,0:T(8,128)(4,1)}, u32[]{:S(2)}) copy-start(pred[64,512]{1,0:T(8,128)(4,1)} %broadcast_compare_fusion) | copy-start | bytes 98308 | tf_op jit(solution)/shard_map/while/body/eval_jaxpr/cond
  54.7 1.6 %copy-start.5 = (s32[1,128,1]{1,2,0:T(1,128)S(1)}, s32[1,128,1]{1,2,0:T(1,128)}, u32[]{:S(2)}) copy-start(s32[1,128,1]{1,2,0:T(1,128)} %param.15) | copy-start | bytes 1540
  85.2 57.0 %all-reduce.5.cloned.1.call-start = ((), (), s32[]{:S(2)}) async-start(), calls=%async_computation.2 | async-start | bytes 163840
  102.5 4.1 %copy-start.6 = (u32[32]{0:T(128)S(1)}, u32[32]{0:T(128)}, u32[]{:S(2)}) copy-start(u32[32]{0:T(128)} %constant.73) | copy-start | bytes 388
Sparse Core Ops, SparseCore 0:
  85.3 16.4 all-reduce.6
  106.7 35.4 all-reduce.4
where the time goes:
time: 158 us
  blocking collectives  57.4 us (36%)
  waiting for transfers between devices  51.1 us (32%)
  matrix products  18.1 us (11%)
  between operations  15.5 us (10%)
  local copies, waits for them, and re-layouts  8.44 us (5%)
  other arithmetic  6.94 us (4%)
    unnamed x3, waiting for transfers between devices  34.5 us
    all_gather x1, blocking collectives, shards(): key_piece = lax.all_gather(keys, 'ctx', axis=1, tiled=True)[0]  16.7 us
    psum x1, waiting for transfers between devices, shards(): lax.psum(up_part.astype(jnp.bfloat16), 'tp').astype(jnp.float32)  16.5 us
    all_gather x1, blocking collectives, shards(): lax.all_gather(values, 'ctx', axis=1, tiled=True)[0]  14.6 us
    all_gather x1, blocking collectives, shards(): gathered = lax.all_gather(arrived[None], 'ctx', axis=0, tiled=True)  13.2 us
    all_to_all x1, blocking collectives, shards(): lax.all_to_all(outgoing.reshape(ep_count, CAP, feature_width), 'ep', spli...  6.44 us
    all_to_all x1, blocking collectives, shards(): lax.all_to_all(expert_rows.reshape(ep_count, CAP, feature_width), 'ep', s...  6.41 us
    dot_general x1, matrix products, shards(): jnp.dot(hidden, down_w, preferred_element_type=jnp.float32)  4.03 us
  transfers between devices with their start and end apart: 2, of which 2 were waited for; matrix products, arithmetic and copies ran while one was open for 0% of the time, Pallas kernels for 0%

commit v1 on v0

--- a/solution.py
+++ b/solution.py
@@ -65,7 +65,7 @@
         fresh_state(half_rows, kv_heads, group_width),
         fresh_state(half_rows, kv_heads, group_width),
     )
-    key_piece = lax.all_gather(keys, "ctx", axis=1, tiled=True)[0]
+    key_piece = jnp.concatenate(lax.all_gather(keys, axis_name="ctx"), axis=1)[0]
     key_count = key_piece.shape[0]
     key_block_rows = block_width(key_count)
     block_count = key_count // key_block_rows

time: 158 us -> 154 us (0.975)
  other arithmetic: 6.94 us -> 3.48 us
  local copies, waits for them, and re-layouts: 8.44 us -> 5.97 us
    add x2, other arithmetic: 2.06 us -> 0.03 us  [absorb_block(): totals = totals * factor + jnp.sum(weights, axis=3)]
    unnamed x13 -> x12, local copies, waits for them, and re-layouts: 3.45 us -> 2.45 us
where the time goes in v1:
time: 154 us
  blocking collectives  58.8 us (38%)
  waiting for transfers between devices  52.1 us (34%)
  matrix products  17.5 us (11%)
  between operations  15.5 us (10%)
  local copies, waits for them, and re-layouts  5.97 us (4%)
  other arithmetic  3.48 us (2%)
    unnamed x3, waiting for transfers between devices  34.5 us
    all_gather x1, blocking collectives, shards(): lax.all_gather(keys, axis_name='ctx')  17.7 us
    psum x1, waiting for transfers between devices, shards(): lax.psum(up_part.astype(jnp.bfloat16), 'tp').astype(jnp.float32)  17.6 us
    all_gather x1, blocking collectives, shards(): lax.all_gather(values, 'ctx', axis=1, tiled=True)[0]  15.1 us
    all_gather x1, blocking collectives, shards(): gathered = lax.all_gather(arrived[None], 'ctx', axis=0, tiled=True)  13.2 us
    all_to_all x1, blocking collectives, shards(): lax.all_to_all(outgoing.reshape(ep_count, CAP, feature_width), 'ep', spli...  6.43 us
    all_to_all x1, blocking collectives, shards(): lax.all_to_all(expert_rows.reshape(ep_count, CAP, feature_width), 'ep', s...  6.41 us
    dot_general x1, matrix products, shards(): jnp.dot(hidden, down_w, preferred_element_type=jnp.float32)  4.03 us
  transfers between devices with their start and end apart: 2, of which 2 were waited for; matrix products, arithmetic and copies ran while one was open for 0% of the time, Pallas kernels for 0%

profile of v1, /device:TPU:0, one launch (start us, length us, event | category | flops | bytes accessed | tf_op | source)
XLA Modules:
  0.0 153.6 jit_solution(426991621969007780)
XLA Ops:
  6.5 0.0 copy-start
  6.5 0.0 all-reduce.7.cloned.1.call-start
  6.6 17.7 %all-gather = bf16[4,128,512]{2,1,0:T(8,128)(2,1)S(1)} all-gather(bf16[1,128,512]{2,1,0:T(8,128)(2,1)} %param.13), channel_id=2, replica_groups=mesh['groups'=2,'ctx'=4,'ep'=2,'tp'=2] {'ctx'}, dimensions={0}, use_global_device_ids=true | all-gather | bytes 655360 | tf_op jit(solution)/shard_map/all_gather | solution.py:68
  24.3 0.1 squeeze.28
  24.4 1.0 copy.22
  25.4 15.1 %all_gather.14 = bf16[1,512,512]{1,2,0:T(8,128)(2,1)S(1)} all-gather(bf16[1,128,512]{1,2,0:T(8,128)(2,1)S(1)} %copy.22), channel_id=1, replica_groups=mesh['groups'=2,'ctx'=4,'ep'=2,'tp'=2] {'ctx'}, dimensions={1}, use_global_device_ids=true | all-gather | bytes 655360 | tf_op jit(solution)/shard_map/all_gather | solution.py:73
  40.5 0.6 slice.23
  41.7 0.1 broadcast.44
  41.8 3.2 %conditional.3 = (f32[4,5,64]{2,1,0:T(8,128)S(1)}, f32[64,4,5,128]{3,0,2,1:T(8,128)S(1)}) conditional(s32[]{:T(128)} %bitcast.13, (f32[4,5,64]{2,1,0:T(8,128)S(1)}, f32[64,4,5,128]{3,0,2,1:T(8,128)S(1)}) %tuple.31, (s32[64]{0:T(128)S(1)}, s32[512]{0:T(512)S(1)}, bf16[1,128,2560]{2,1,0:T(8,128)(2,1)S(1)}, bf16[512,4,128]{2,1,0:T(4,128)(2,1)S(1)}, ...), branch_computations={%region_4.5_spmd, %region_5.0_spmd} | conditional | flops 344428288 | bytes 12067088 | solution.py:89
  41.9 0.1 broadcast_compare_fusion.1
  42.0 0.4 slice.19
  42.4 0.7 fusion.20
  43.1 0.9 fusion.22
  44.0 1.1 fusion.29
  45.1 0.2 divide_convert_fusion
  45.3 0.2 copy.28
  45.6 0.4 reshape.57
  45.9 0.6 slice.22
  47.2 3.2 %conditional.2 = ((f32[4,5,64]{2,1,0:T(8,128)S(1)}, f32[64,4,5,128]{3,0,2,1:T(8,128)S(1)})) conditional(s32[]{:T(128)} %bitcast.10, (f32[4,5,64]{2,1,0:T(8,128)S(1)}, f32[64,4,5,128]{3,0,2,1:T(8,128)S(1)}) %tuple.31, (s32[64]{0:T(128)S(1)}, s32[512]{0:T(512)S(1)}, bf16[1,128,2560]{2,1,0:T(8,128)(2,1)S(1)}, bf16[512,4,128]{2,1,0:T(4,128)(2,1)S(1)}, ...), branch_computations={%region_0.1_spmd, %region_1.4_spmd} | conditional | flops 344428288 | bytes 12067096 | solution.py:81
  47.2 0.1 broadcast_compare_fusion
  47.3 0.4 slice.17
  47.7 0.7 fusion
  48.5 0.9 fusion.2
  49.3 1.1 fusion.9
  50.4 0.0 copy-start.2
  50.4 0.2 divide_convert_fusion.1
  50.7 0.2 copy.25
  50.9 0.4 reshape.56
  51.3 0.1 fusion.59
  51.4 0.2 reduce_window_sum.11
  51.6 0.2 select_reduce_fusion
  51.8 0.2 convolution_convert_fusion
  52.0 6.4 %all_to_all.10 = bf16[2,2,2560]{2,1,0:T(2,128)(2,1)S(1)} all-to-all(bf16[2,2,2560]{2,1,0:T(2,128)(2,1)S(1)} %reshape.58), channel_id=1, replica_groups=mesh['groups'=2,'ctx'=4,'ep'=2,'tp'=2] {'ep'}, dimensions={0} | all-to-all | bytes 40960 | tf_op jit(solution)/shard_map/all_to_all | solution.py:113
  58.5 13.2 %all-gather.1 = bf16[8,2,2560]{2,1,0:T(2,128)(2,1)S(1)} all-gather(bf16[2,2,2560]{2,1,0:T(2,128)(2,1)S(1)} %all_to_all.10), channel_id=3, replica_groups=mesh['groups'=2,'ctx'=4,'ep'=2,'tp'=2] {'ctx'}, dimensions={0}, use_global_device_ids=true | all-gather | bytes 102400 | tf_op jit(solution)/shard_map/all_gather | solution.py:120
  71.7 3.9 %fusion.51 = bf16[16,1024]{1,0:T(8,128)(2,1)} fusion(bf16[16,2560]{1,0:T(8,128)(2,1)S(1)} %reshape.59, bf16[1,2560,1024]{2,1,0:T(8,128)(2,1)} %param.17), kind=kOutput, calls=%fused_computation.51 | convolution fusion | flops 83902464 | bytes 5357568 | tf_op jit(solution)/shard_map/dot_general | solution.py:125
  75.6 3.9 %fusion.54 = bf16[16,1024]{1,0:T(8,128)(2,1)} fusion(bf16[16,2560]{1,0:T(8,128)(2,1)S(1)} %reshape.59, bf16[1,2560,1024]{2,1,0:T(8,128)(2,1)} %param.18), kind=kOutput, calls=%fused_computation.52 | convolution fusion | flops 83902464 | bytes 5357568 | tf_op jit(solution)/shard_map/dot_general | solution.py:126
  79.5 0.7 fusion.58
  80.2 0.0 all-reduce.7.cloned.1.call-update
  80.2 0.0 all-reduce.5.cloned.1.call-start
  80.3 17.6 %all-reduce.7.cloned.1.call-done = (bf16[16,1024]{1,0:T(8,128)(2,1)}, bf16[16,1024]{1,0:T(8,128)(2,1)}, bf16[16,1]{0,1:T(2,128)(2,1)}) async-done(((bf16[16,1024]{1,0:T(8,128)(2,1)}, bf16[16,1024]{1,0:T(8,128)(2,1)}, bf16[16,1]{0,1:T(2,128)(2,1)}), (bf16[16,1024]{1,0:T(8,128)(2,1)}, bf16[16,1024]{1,0:T(8,128)(2,1)}, bf16[16,1]{0,1:T(2,128)(2,1)})) %all-reduce.7.cloned.1.call-update) | async-done | bytes 65584 | tf_op jit(solution)/shard_map/psum | solution.py:130
  97.9 0.6 divide_bitcast_fusion
  98.5 4.0 %fusion.48 = bf16[16,2560]{1,0:T(8,128)(2,1)} fusion(bf16[1,1024,2560]{2,1,0:T(8,128)(2,1)} %param.19, bf16[16,1024]{1,0:T(8,128)(2,1)} %get-tuple-element.178, bf16[16,1024]{1,0:T(8,128)(2,1)} %get-tuple-element.179, f32[16]{0:T(128)S(1)} %divide_bitcast_fusion), kind=kOutput, calls=%fused_computation.49 | convolution fusion | flops 84090880 | bytes 5390400 | tf_op jit(solution)/shard_map/dot_general | solution.py:136
  102.6 0.0 all-reduce.5.cloned.1.call-update
  102.6 0.6 dynamic-slice
  103.8 34.4 %all-reduce.5.cloned.1.call-done = bf16[16,2560]{1,0:T(8,128)(2,1)} async-done(((bf16[16,2560]{1,0:T(8,128)(2,1)}), bf16[16,2560]{1,0:T(8,128)(2,1)}) %all-reduce.5.cloned.1.call-update) | async-done | bytes 81936
  138.2 0.8 constant_dynamic-slice_fusion
  139.0 6.4 %all_to_all.11 = bf16[2,2,2560]{2,1,0:T(2,128)(2,1)S(1)} all-to-all(bf16[2,2,2560]{2,1,0:T(2,128)(2,1)S(1)} %reshape.61), channel_id=1, replica_groups=mesh['groups'=2,'ctx'=4,'ep'=2,'tp'=2] {'ep'}, dimensions={0} | all-to-all | bytes 40960 | tf_op jit(solution)/shard_map/all_to_all | solution.py:141
  145.5 1.2 fusion.47
  (25 shorter events, 0.3 us)
Async XLA Ops:
  6.5 73.0 %copy-start = (bf16[2560,1]{0,1:T(2,128)(2,1)S(1)}, bf16[2560,1]{0,1:T(2,128)(2,1)}, u32[]{:S(2)}) copy-start(bf16[2560,1]{0,1:T(2,128)(2,1)} %param.16) | copy-start | bytes 15364
  6.5 35.3 %copy-start.1 = (bf16[1,128,2560]{2,1,0:T(8,128)(2,1)S(1)}, bf16[1,128,2560]{2,1,0:T(8,128)(2,1)}, u32[]{:S(2)}) copy-start(bf16[1,128,2560]{2,1,0:T(8,128)(2,1)} %param.12) | copy-start | bytes 1966084
  6.5 91.4 %all-reduce.7.cloned.1.call-start = ((), (), s32[]{:S(2)}) async-start(), calls=%async_computation.3 | async-start | bytes 132096 | tf_op jit(solution)/shard_map/psum | solution.py:130
  50.4 0.9 copy-start.2
  80.2 58.0 %all-reduce.5.cloned.1.call-start = ((), (), s32[]{:S(2)}) async-start(), calls=%async_computation.2 | async-start | bytes 163840
  98.5 4.1 %copy-start.3 = (u32[32]{0:T(128)S(1)}, u32[32]{0:T(128)}, u32[]{:S(2)}) copy-start(u32[32]{0:T(128)} %constant.73) | copy-start | bytes 388
Sparse Core Ops, SparseCore 0:
  80.4 17.4 all-reduce.6
  102.7 35.4 all-reduce.4
